TPU v7x, 256 devices: a whole 4x4x8 slice. The times are simulated.
256 devices in a mesh: gx: 64 (over x, y_lo, z), gy: 4 (over y_hi, core).
Axes of the slice: x: 4, y: 4 (y_hi: 2, y_lo: 2; y = y_hi * 2 + y_lo), z: 8, core: 2. Of those that a mesh axis runs over, the one named last changes fastest.
Arguments:
- state: float32 [12, 4, 256, 8192], P(None, None, 'gy', 'gx'), may hold values from -240 to 240, as said below
- inverse: float32 [128, 256, 256], P('gy'), may hold values from -0.6 to 1.8, as said below
Outputs:
- updated: float32 [12, 4, 256, 8192], P(None, None, 'gy', 'gx')
- wall_stress: float32 [12, 2, 2, 8192], P(None, None, None, 'gx')
Inputs may be any that keep to these rules, and one draw needn't show every extreme that they name: `state`: perturbation coefficients, of varying size over coefficients and x. Each inverse is a dense matrix with a positive diagonal.
All inputs are finite; a program needn't handle non-finite values.
Results may differ from a plain program's by a relative error of at most 0.0003.
Values sent between devices are 32-bit elements; how exact they have to be, the bound alone decides.
A program may use at most 64 MiB of HBM per device.

v0:
```python
import functools

import jax
import jax.numpy as jnp
import numpy as np
from jax import lax
from jax.experimental import pallas as pl
from jax.experimental.pallas import tpu as pltpu
from jax.sharding import Mesh
from jax.sharding import PartitionSpec as P

MODES = 128
HALO = 64
AXES = ("gx_0", "gx_1", "gx_2", "gy_0", "gy_1")
GX = ("gx_0", "gx_1", "gx_2")
GY = ("gy_0", "gy_1")
EPSILON = 1e-06
TIME_STEP = 0.5
MEAN_FLOW = 0.8
CORIOLIS = 0.6
STRATIFICATION = 0.9
F32 = jnp.float32
BF16 = jnp.bfloat16
MESH = pl.DeviceIdType.MESH

MEMBERS = 12
FIELDS = 4
LOCAL = 64
PTS = 128
QUARTER = 32
BLOCK = 2 * QUARTER
STEP = 2
STEPS = MEMBERS // STEP
GROUP = 4
GROUPS = MEMBERS // GROUP
UNROLL = 8


def window_tables(window, rim, points, modes):
    pos = np.arange(window)
    mode = np.arange(modes)
    half = modes // 2
    cosine = mode <= half
    wave = np.where(cosine, mode, mode - half)
    phase = 2.0 * np.pi * (pos[:, None] * wave[None, :] % window) / window
    norm = np.where(wave == 0, np.sqrt(1.0 / window), np.sqrt(2.0 / window))
    basis = np.where(cosine[None, :], np.cos(phase), np.sin(phase)) * norm[None, :]
    kappa = 2.0 * np.pi * wave / window
    paired = wave[:, None] == wave[None, :]
    to_sine = cosine[:, None] & ~cosine[None, :] & paired
    to_cosine = ~cosine[:, None] & cosine[None, :] & paired
    derivative = np.where(to_sine, -kappa[:, None], 0.0) + np.where(to_cosine, kappa[:, None], 0.0)
    taper = 0.25 + 0.75 * np.sin(np.pi * (pos + 0.5) / window) ** 2
    plain = basis * taper[:, None]
    slope = (basis @ derivative) * taper[:, None]
    both = np.concatenate([plain - TIME_STEP * MEAN_FLOW * slope, plain], axis=1).T
    order = np.concatenate([np.arange(rim, window), np.arange(rim)])
    back = (basis[rim : rim + points] / taper[rim : rim + points, None]).T
    return both[:, order], back


def split_table(table):
    high = table.astype(BF16)
    low = (table - high.astype(np.float64)).astype(BF16)
    return high, low


def split(a):
    high = a.astype(BF16)
    low = (a - high.astype(F32)).astype(BF16)
    return high, low


def dot_t(a, b):
    return lax.dot_general(a, b, (((1,), (1,)), ((), ())), preferred_element_type=F32)


def dot(a, b):
    return lax.dot_general(a, b, (((1,), (0,)), ((), ())), preferred_element_type=F32)


def kernel(
    sizes,
    state_hbm, inverse_hbm, project_hbm, back_hbm, out_ref, wall_ref,
    state, inverse, inv_high, inv_low, project, back,
    to_right, to_left, from_left, from_right,
    out_modes, in_modes, out_coefs, in_coefs,
    sum_mine, sum_theirs, wall_mine, wall_all,
    local_sem, halo_send, halo_recv, mode_send, mode_recv, coef_send, coef_recv,
    sum_send, sum_recv, wall_send, wall_recv,
):
    nx, ny, nz = sizes
    x, y, z = (lax.axis_index(a) for a in GX)
    hi, core = (lax.axis_index(a) for a in GY)
    me = hi * 2 + core
    count = nx * ny * nz
    here = (x * ny + y) * nz + z

    def place(index):
        return {
            "gx_0": lax.div(index, ny * nz),
            "gx_1": lax.rem(lax.div(index, nz), ny),
            "gx_2": lax.rem(index, nz),
        }

    right = place(lax.rem(here + 1, count))
    left = place(lax.rem(here + count - 1, count))
    solvers = [{"gx_1": 1 - y, "gy_0": q // 2, "gy_1": q % 2} for q in range(4)]

    def other(step):
        index = lax.rem(me + step, 4)
        return index, {"gy_0": lax.div(index, 2), "gy_1": lax.rem(index, 2)}

    partners = [{"gy_1": 1 - core}, {"gx_1": 1 - y}, {"gy_0": 1 - hi}]
    for name, value, size in (("gx_0", x, nx), ("gx_2", z, nz)):
        bit = 1
        while bit < size:
            flip = value + bit - 2 * bit * lax.rem(lax.div(value, bit), 2)
            partners.append({name: flip})
            bit *= 2
    rounds = len(partners)

    barrier = pltpu.get_barrier_semaphore()
    met = [right, left, *solvers, other(1)[1], other(2)[1], other(3)[1], *partners[3:]]
    for device in met:
        pl.semaphore_signal(barrier, inc=1, device_id=device, device_id_type=MESH)

    loads = [
        pltpu.make_async_copy(state_hbm, state, local_sem.at[0]),
        pltpu.make_async_copy(project_hbm, project, local_sem.at[1]),
        pltpu.make_async_copy(back_hbm, back, local_sem.at[2]),
    ]
    for k in range(4):
        part = pl.ds(k * 8, 8)
        loads.append(
            pltpu.make_async_copy(inverse_hbm.at[part], inverse.at[part], local_sem.at[3 + k])
        )
    for load in loads:
        load.start()

    lane = lax.broadcasted_iota(jnp.int32, (1, PTS), 1)
    low_half = lane < LOCAL

    def halo_copies(step):
        rows = pl.ds(step * STEP, STEP)
        return (
            pltpu.make_async_remote_copy(
                to_right.at[rows], from_left.at[rows], halo_send.at[0, step], halo_recv.at[0, step],
                device_id=right, device_id_type=MESH,
            ),
            pltpu.make_async_remote_copy(
                to_left.at[rows], from_right.at[rows], halo_send.at[1, step], halo_recv.at[1, step],
                device_id=left, device_id_type=MESH,
            ),
        )

    loads[0].wait()

    def pack(e):
        centre = state[e]
        top, low = centre[:, :32], centre[:, 32:]
        turned = pltpu.roll(low, LOCAL, 2)
        to_right[e] = jnp.where(low_half, turned, top)
        to_left[e] = jnp.where(low_half, top, turned)

    pack(0)
    pack(1)
    pl.semaphore_wait(barrier, len(met))
    for copy in halo_copies(0):
        copy.start()

    def pack_and_send(step, carry):
        pack(step * STEP)
        pack(step * STEP + 1)
        for copy in halo_copies(step):
            copy.start()
        return carry

    lax.fori_loop(1, STEPS, pack_and_send, 0)

    sum_mine[0] = jnp.zeros((16, PTS), F32)

    def squares(e, carry):
        values = state[e].reshape(FIELDS * LOCAL, PTS)
        sum_mine[0, pl.ds(e, 1), :] = jnp.sum(values * values, axis=0, keepdims=True)
        return carry

    lax.fori_loop(0, MEMBERS, squares, 0)

    def sum_copy(k):
        return pltpu.make_async_remote_copy(
            sum_mine.at[k], sum_theirs.at[k], sum_send.at[k], sum_recv.at[k],
            device_id=partners[k], device_id_type=MESH,
        )

    sum_copy(0).start()

    def sum_round(k):
        sum_copy(k).wait_recv()
        sum_mine[k + 1] = sum_mine[k] + sum_theirs[k]
        if k + 1 < rounds:
            sum_copy(k + 1).start()

    for load in loads[1:]:
        load.wait()

    def split_inverse(m, carry):
        high, low = split(inverse[m])
        inv_high[m] = high
        inv_low[m] = low
        return carry

    lax.fori_loop(0, QUARTER, split_inverse, 0)

    coupling_0 = jnp.where(low_half, TIME_STEP * CORIOLIS, TIME_STEP)
    coupling_1 = jnp.where(low_half, -TIME_STEP * CORIOLIS, -TIME_STEP * STRATIFICATION)
    coefficient = me * LOCAL + lax.rem(lane, LOCAL)
    interior = coefficient < 4 * LOCAL - 2

    def mode_copies(step):
        rows = pl.ds(step * (STEP * BLOCK), STEP * BLOCK)
        return [
            pltpu.make_async_remote_copy(
                out_modes.at[q, rows], in_modes.at[me, rows],
                mode_send.at[q, step], mode_recv.at[me, step],
                device_id=solvers[q], device_id_type=MESH,
            )
            for q in range(4)
        ]

    def project_member(e):
        centre = state[e]
        rim_left, rim_right = from_left[e], from_right[e]
        top = jnp.where(low_half, rim_right, rim_left)
        low = pltpu.roll(jnp.where(low_half, rim_left, rim_right), LOCAL, 2)
        rim = jnp.concatenate([top, low], axis=1)
        segment = jnp.concatenate(
            [centre.reshape(FIELDS * LOCAL, PTS), rim.reshape(FIELDS * LOCAL, PTS)], axis=1
        )
        high, low = split(segment)
        first = dot_t(project[...], high)
        second = dot_t(project[: 2 * MODES], low)
        both = first[: 2 * MODES] + (first[2 * MODES :] + second)
        a_0, a_1 = both[:MODES, :PTS], both[:MODES, PTS:]
        b_0, b_1 = both[MODES:, :PTS], both[MODES:, PTS:]
        rhs_0 = jnp.where(interior, a_0 + coupling_0 * b_1, 0.0)
        rhs_1 = jnp.where(interior, a_1 + coupling_1 * b_0, 0.0)
        for q in range(4):
            modes = slice(q * QUARTER, (q + 1) * QUARTER)
            base = pl.multiple_of(e * BLOCK, BLOCK)
            out_modes[q, pl.ds(base, QUARTER), :] = rhs_0[modes]
            out_modes[q, pl.ds(base + QUARTER, QUARTER), :] = rhs_1[modes]

    def project_step(step, carry):
        for copy in halo_copies(step):
            copy.wait_recv()
        for k in range(STEP):
            project_member(step * STEP + k)
        for copy in mode_copies(step):
            copy.start()
        for k in range(min(rounds, STEPS)):
            @pl.when(step == k)
            def _():
                sum_round(k)
        return carry

    lax.fori_loop(0, STEPS, project_step, 0)
    for k in range(STEPS, rounds):
        sum_round(k)

    def coef_copies(group):
        rows = pl.ds(group * (GROUP * BLOCK), GROUP * BLOCK)
        return [
            pltpu.make_async_remote_copy(
                out_coefs.at[t, rows], in_coefs.at[me, rows],
                coef_send.at[t, group], coef_recv.at[me, group],
                device_id=solvers[t], device_id_type=MESH,
            )
            for t in range(4)
        ]

    def arrived(buffer, sem, rows, s, k):
        return pltpu.make_async_remote_copy(
            buffer.at[s, rows], buffer.at[s, rows], sem.at[s, k], sem.at[s, k],
            device_id=solvers[s], device_id_type=MESH,
        )

    def turn(a):
        return pltpu.roll(a, LOCAL, 1)

    def solve_mode(base, m):
        rows = pl.ds(base + m, 2 * GROUP, stride=QUARTER)
        parts = [in_modes[s, rows, :] for s in range(4)]
        even, odd = [], []
        for s in (0, 2):
            first, second = parts[s], parts[s + 1]
            even.append(jnp.where(low_half, first, turn(second)))
            odd.append(jnp.where(low_half, turn(first), second))
        values = jnp.concatenate(
            [jnp.concatenate(even, axis=1), jnp.concatenate(odd, axis=1)], axis=0
        )
        high, low = split(values)
        count = 4 * GROUP
        first = dot_t(jnp.concatenate([high, low], axis=0), inv_high[m])
        second = dot_t(high, inv_low[m])
        solved = first[:count] + (first[count:] + second)
        even, odd = solved[: 2 * GROUP], solved[2 * GROUP :]
        for k in range(2):
            lanes = slice(k * PTS, (k + 1) * PTS)
            out_coefs[2 * k, rows, :] = jnp.where(low_half, even[:, lanes], turn(odd[:, lanes]))
            out_coefs[2 * k + 1, rows, :] = jnp.where(low_half, turn(even[:, lanes]), odd[:, lanes])

    def solve_group(group, carry):
        for s in range(4):
            for k in range(GROUP // STEP):
                step = group * (GROUP // STEP) + k
                rows = pl.ds(step * (STEP * BLOCK), STEP * BLOCK)
                arrived(in_modes, mode_recv, rows, s, step).wait_recv()
        base = group * (GROUP * BLOCK)

        def some_modes(k, carry):
            for u in range(UNROLL):
                solve_mode(base, k * UNROLL + u)
            return carry

        lax.fori_loop(0, QUARTER // UNROLL, some_modes, 0)
        for copy in coef_copies(group):
            copy.start()
        return carry

    lax.fori_loop(0, GROUPS, solve_group, 0)

    row = lax.broadcasted_iota(jnp.int32, (LOCAL, PTS), 0)
    k_float = (me * LOCAL + row).astype(F32)
    curvature = k_float * k_float / float((4 * LOCAL) ** 2)
    parity = jnp.where(lax.rem(row[:8], 2) == 0, -1.0, 1.0)
    grid = float(FIELDS * 4 * LOCAL * PTS * count)

    def back_member(e):
        base = pl.multiple_of(e * BLOCK, BLOCK)
        turned = []
        for col in range(2):
            block = jnp.concatenate(
                [in_coefs[q, pl.ds(base + col * QUARTER, QUARTER), :] for q in range(4)], axis=0
            )
            turned.append(block.T)
        high, low = split(jnp.concatenate(turned, axis=0))
        values = dot(jnp.concatenate([high, low], axis=1), back[: 2 * MODES])
        values = values + dot(high, back[2 * MODES :])
        total = jnp.sum(sum_mine[rounds, pl.ds(e, 1), :], axis=1, keepdims=True)
        values = values * lax.rsqrt(total / grid + EPSILON)
        out_ref[e] = values.reshape(FIELDS, LOCAL, PTS)
        for c in range(2):
            weighted = values[c * PTS : c * PTS + LOCAL] * curvature
            rows = jnp.sum(weighted.reshape(LOCAL // 8, 8, PTS), axis=0)
            wall_mine[pl.ds(e * 4 + c, 1), :] = jnp.sum(rows, axis=0, keepdims=True)
            wall_mine[pl.ds(e * 4 + 2 + c, 1), :] = jnp.sum(rows * parity, axis=0, keepdims=True)

    def back_group(group, carry):
        rows = pl.ds(group * (GROUP * BLOCK), GROUP * BLOCK)
        for s in range(4):
            arrived(in_coefs, coef_recv, rows, s, group).wait_recv()

        def one(k, carry):
            back_member(group * GROUP + k)
            return carry

        lax.fori_loop(0, GROUP, one, 0)
        return carry

    lax.fori_loop(0, GROUPS, back_group, 0)

    def wall_copy(step):
        index, device = other(step)
        send = pltpu.make_async_remote_copy(
            wall_mine, wall_all.at[me], wall_send.at[step - 1], wall_recv.at[me],
            device_id=device, device_id_type=MESH,
        )
        receive = pltpu.make_async_remote_copy(
            wall_mine, wall_all.at[index], wall_send.at[step - 1], wall_recv.at[index],
            device_id=device, device_id_type=MESH,
        )
        return send, receive

    for step in (1, 2, 3):
        wall_copy(step)[0].start()
    wall_all[me] = wall_mine[...]

    def ended(step, carry):
        for copy in halo_copies(step):
            copy.wait_send()
        for copy in mode_copies(step):
            copy.wait_send()
        return carry

    lax.fori_loop(0, STEPS, ended, 0)

    def ended_group(group, carry):
        for copy in coef_copies(group):
            copy.wait_send()
        return carry

    lax.fori_loop(0, GROUPS, ended_group, 0)
    for k in range(rounds):
        sum_copy(k).wait_send()
    for step in (1, 2, 3):
        wall_copy(step)[0].wait_send()
        wall_copy(step)[1].wait_recv()
    wall_ref[...] = (wall_all[0] + wall_all[1]) + (wall_all[2] + wall_all[3])


def per_device(sizes, state, inverse):
    both, back = window_tables(PTS + 2 * HALO, HALO, PTS, MODES)
    project = jnp.asarray(np.concatenate(split_table(both), axis=0))
    high, low = split_table(back)
    back = jnp.asarray(np.concatenate([high, high, low], axis=0))
    rounds = 3 + (sizes[0].bit_length() - 1) + (sizes[2].bit_length() - 1)
    exchange = (4, MEMBERS * BLOCK, PTS)
    rim = (MEMBERS, FIELDS, 32, PTS)
    vmem = pltpu.VMEM
    dma = pltpu.SemaphoreType.DMA
    updated, wall = pl.pallas_call(
        functools.partial(kernel, sizes),
        out_shape=(
            jax.ShapeDtypeStruct(state.shape, F32),
            jax.ShapeDtypeStruct((4 * MEMBERS, PTS), F32),
        ),
        in_specs=[pl.BlockSpec(memory_space=pl.ANY)] * 4,
        out_specs=(
            pl.BlockSpec(memory_space=pltpu.VMEM),
            pl.BlockSpec(memory_space=pltpu.VMEM),
        ),
        scratch_shapes=[
            vmem(state.shape, F32),
            vmem(inverse.shape, F32),
            vmem(inverse.shape, BF16),
            vmem(inverse.shape, BF16),
            vmem(project.shape, BF16),
            vmem(back.shape, BF16),
            *[vmem(rim, F32)] * 4,
            *[vmem(exchange, F32)] * 4,
            vmem((rounds + 1, 16, PTS), F32),
            vmem((rounds, 16, PTS), F32),
            vmem((4 * MEMBERS, PTS), F32),
            vmem((4, 4 * MEMBERS, PTS), F32),
            dma((7,)),
            dma((2, STEPS)),
            dma((2, STEPS)),
            dma((4, STEPS)),
            dma((4, STEPS)),
            dma((4, GROUPS)),
            dma((4, GROUPS)),
            dma((rounds,)),
            dma((rounds,)),
            dma((3,)),
            dma((4,)),
        ],
        compiler_params=pltpu.CompilerParams(
            collective_id=0, has_side_effects=True, vmem_limit_bytes=56 * 1024 * 1024
        ),
        name="step",
    )(state, inverse, project, back)
    return updated, wall.reshape(MEMBERS, 2, 2, PTS)


def solution(mesh):
    torus = Mesh(mesh.devices.reshape(4, 2, 8, 2, 2), AXES)
    return jax.shard_map(
        functools.partial(per_device, (4, 2, 8)),
        mesh=torus,
        in_specs=(P(None, None, GY, GX), P(GY, None, None)),
        out_specs=(P(None, None, GY, GX), P(None, None, None, GX)),
        check_vma=False,
    )
```

profile of v0, /device:TPU:1, one launch (start us, length us, event | category | flops | bytes accessed | tf_op | source)
XLA Modules:
  0.0 82.1 jit_solution(9511094775472291962)
XLA Ops:
  0.6 78.1 %step.1 = (f32[12,4,64,128]{3,2,1,0:T(8,128)}, f32[48,128]{1,0:T(8,128)}) custom-call(f32[12,4,64,128]{3,2,1,0:T(8,128)} %state_hbm.1, f32[32,256,256]{2,1,0:T(8,128)} %inverse_hbm.1, bf16[512,256]{1,0:T(8,128)(2,1)} %constant.4.clone.project_hbm, bf16[384,128]{1,0:T(8,128)(2,1)} %constant.5.clone.back_hbm), custom_call_target="tpu_custom_call" | custom-call | tf_op jit(solution)/shard_map/step/pallas_call | solution.py:422
  78.8 0.0 copy-start
  78.8 2.7 %copy.8 = f32[12,4,64,128]{3,2,1,0:T(8,128)} copy(f32[12,4,64,128]{3,2,1,0:T(8,128)} %get-tuple-element.8) | data formatting | bytes 3145728
  81.5 0.0 copy-done
  81.5 0.6 copy.9
Async XLA Ops:
  78.8 2.7 %copy-start = (f32[48,128]{1,0:T(8,128)S(1)}, f32[48,128]{1,0:T(8,128)}, u32[]{:S(2)}) copy-start(f32[48,128]{1,0:T(8,128)} %get-tuple-element.5) | copy-start | bytes 73732
where the time goes:
time: 82.9 us; the launch traced here: 82.1 us
  Pallas kernels  78.1 us (94%)
  local copies, waits for them, and re-layouts  3.34 us (4%)
    pallas_call x1, Pallas kernels, per_device(): pl.pallas_call(functools.partial(kernel, sizes), out_shape=(jax.ShapeDtyp...  78.1 us
    unnamed x4, local copies, waits for them, and re-layouts  3.34 us

commit v1 on v0

--- a/solution.py
+++ b/solution.py
@@ -85,7 +85,7 @@
     state, inverse, inv_high, inv_low, project, back,
     to_right, to_left, from_left, from_right,
     out_modes, in_modes, out_coefs, in_coefs,
-    sum_mine, sum_theirs, wall_mine, wall_all,
+    sum_mine, sum_all, wall_mine, wall_all,
     local_sem, halo_send, halo_recv, mode_send, mode_recv, coef_send, coef_recv,
     sum_send, sum_recv, wall_send, wall_recv,
 ):
@@ -111,22 +111,32 @@
         index = lax.rem(me + step, 4)
         return index, {"gy_0": lax.div(index, 2), "gy_1": lax.rem(index, 2)}
 
-    partners = [{"gy_1": 1 - core}, {"gx_1": 1 - y}, {"gy_0": 1 - hi}]
-    for name, value, size in (("gx_0", x, nx), ("gx_2", z, nz)):
-        bit = 1
-        while bit < size:
-            flip = value + bit - 2 * bit * lax.rem(lax.div(value, bit), 2)
-            partners.append({name: flip})
-            bit *= 2
-    rounds = len(partners)
+    def stage_peer(stage, step):
+        if stage == 0:
+            index = lax.rem(z + step, nz)
+            return index, {"gx_2": index}
+        if stage == 1:
+            index = lax.rem(x + step, nx)
+            return index, {"gx_0": index}
+        index = lax.rem(y * 4 + me + step, 4 * ny)
+        return index, {
+            "gx_1": lax.div(index, 4),
+            "gy_0": lax.rem(lax.div(index, 2), 2),
+            "gy_1": lax.rem(index, 2),
+        }
+
+    stage_me = (z, x, y * 4 + me)
+    stage_size = (nz, nx, 4 * ny)
+    peers = [stage_peer(k, n)[1] for k in range(3) for n in range(1, stage_size[k])]
 
     barrier = pltpu.get_barrier_semaphore()
-    met = [right, left, *solvers, other(1)[1], other(2)[1], other(3)[1], *partners[3:]]
+    met = [right, left, *peers]
     for device in met:
         pl.semaphore_signal(barrier, inc=1, device_id=device, device_id_type=MESH)
 
+    state_load = pltpu.make_async_copy(state_hbm, state, local_sem.at[0])
+    state_load.start()
     loads = [
-        pltpu.make_async_copy(state_hbm, state, local_sem.at[0]),
         pltpu.make_async_copy(project_hbm, project, local_sem.at[1]),
         pltpu.make_async_copy(back_hbm, back, local_sem.at[2]),
     ]
@@ -135,8 +145,6 @@
         loads.append(
             pltpu.make_async_copy(inverse_hbm.at[part], inverse.at[part], local_sem.at[3 + k])
         )
-    for load in loads:
-        load.start()
 
     lane = lax.broadcasted_iota(jnp.int32, (1, PTS), 1)
     low_half = lane < LOCAL
@@ -154,7 +162,9 @@
             ),
         )
 
-    loads[0].wait()
+    state_load.wait()
+    for load in loads:
+        load.start()
 
     def pack(e):
         centre = state[e]
@@ -163,45 +173,56 @@
         to_right[e] = jnp.where(low_half, turned, top)
         to_left[e] = jnp.where(low_half, top, turned)
 
-    pack(0)
-    pack(1)
+    for k in range(STEP):
+        pack(k)
+
+    def squares(e, carry):
+        values = state[e].reshape(FIELDS * LOCAL, PTS)
+        total = jnp.sum(values * values, axis=0, keepdims=True)
+        return jnp.where(lane == e, jnp.sum(total, axis=1, keepdims=True), carry)
+
+    sum_mine[0] = lax.fori_loop(0, MEMBERS, squares, jnp.zeros((1, PTS), F32))
+
+    def sum_copies(stage, step):
+        index, device = stage_peer(stage, step)
+
+        def copy(slot):
+            return pltpu.make_async_remote_copy(
+                sum_mine.at[stage], sum_all.at[stage, slot],
+                sum_send.at[stage, step - 1], sum_recv.at[stage, slot],
+                device_id=device, device_id_type=MESH,
+            )
+
+        return copy(stage_me[stage]), copy(index)
+
+    def sum_start(stage):
+        for step in range(1, stage_size[stage]):
+            sum_copies(stage, step)[0].start()
+        sum_all[stage, stage_me[stage]] = sum_mine[stage]
+
+    def sum_end(stage):
+        for step in range(1, stage_size[stage]):
+            sum_copies(stage, step)[1].wait_recv()
+        total = sum_all[stage, 0]
+        for k in range(1, stage_size[stage]):
+            total = total + sum_all[stage, k]
+        sum_mine[stage + 1] = total
+
     pl.semaphore_wait(barrier, len(met))
+    sum_start(0)
     for copy in halo_copies(0):
         copy.start()
 
     def pack_and_send(step, carry):
-        pack(step * STEP)
-        pack(step * STEP + 1)
+        for k in range(STEP):
+            pack(step * STEP + k)
         for copy in halo_copies(step):
             copy.start()
         return carry
 
     lax.fori_loop(1, STEPS, pack_and_send, 0)
 
-    sum_mine[0] = jnp.zeros((16, PTS), F32)
-
-    def squares(e, carry):
-        values = state[e].reshape(FIELDS * LOCAL, PTS)
-        sum_mine[0, pl.ds(e, 1), :] = jnp.sum(values * values, axis=0, keepdims=True)
-        return carry
-
-    lax.fori_loop(0, MEMBERS, squares, 0)
-
-    def sum_copy(k):
-        return pltpu.make_async_remote_copy(
-            sum_mine.at[k], sum_theirs.at[k], sum_send.at[k], sum_recv.at[k],
-            device_id=partners[k], device_id_type=MESH,
-        )
-
-    sum_copy(0).start()
-
-    def sum_round(k):
-        sum_copy(k).wait_recv()
-        sum_mine[k + 1] = sum_mine[k] + sum_theirs[k]
-        if k + 1 < rounds:
-            sum_copy(k + 1).start()
-
-    for load in loads[1:]:
+    for load in loads:
         load.wait()
 
     def split_inverse(m, carry):
@@ -258,15 +279,20 @@
             project_member(step * STEP + k)
         for copy in mode_copies(step):
             copy.start()
-        for k in range(min(rounds, STEPS)):
-            @pl.when(step == k)
-            def _():
-                sum_round(k)
+
+        @pl.when(step == 2)
+        def _():
+            sum_end(0)
+            sum_start(1)
+
+        @pl.when(step == 4)
+        def _():
+            sum_end(1)
+            sum_start(2)
+
         return carry
 
     lax.fori_loop(0, STEPS, project_step, 0)
-    for k in range(STEPS, rounds):
-        sum_round(k)
 
     def coef_copies(group):
         rows = pl.ds(group * (GROUP * BLOCK), GROUP * BLOCK)
@@ -335,6 +361,8 @@
     curvature = k_float * k_float / float((4 * LOCAL) ** 2)
     parity = jnp.where(lax.rem(row[:8], 2) == 0, -1.0, 1.0)
     grid = float(FIELDS * 4 * LOCAL * PTS * count)
+
+    sum_end(2)
 
     def back_member(e):
         base = pl.multiple_of(e * BLOCK, BLOCK)
@@ -347,7 +375,7 @@
         high, low = split(jnp.concatenate(turned, axis=0))
         values = dot(jnp.concatenate([high, low], axis=1), back[: 2 * MODES])
         values = values + dot(high, back[2 * MODES :])
-        total = jnp.sum(sum_mine[rounds, pl.ds(e, 1), :], axis=1, keepdims=True)
+        total = jnp.sum(jnp.where(lane == e, sum_mine[3], 0.0), axis=1, keepdims=True)
         values = values * lax.rsqrt(total / grid + EPSILON)
         out_ref[e] = values.reshape(FIELDS, LOCAL, PTS)
         for c in range(2):
@@ -401,8 +429,9 @@
         return carry
 
     lax.fori_loop(0, GROUPS, ended_group, 0)
-    for k in range(rounds):
-        sum_copy(k).wait_send()
+    for stage in range(3):
+        for step in range(1, stage_size[stage]):
+            sum_copies(stage, step)[0].wait_send()
     for step in (1, 2, 3):
         wall_copy(step)[0].wait_send()
         wall_copy(step)[1].wait_recv()
@@ -414,7 +443,6 @@
     project = jnp.asarray(np.concatenate(split_table(both), axis=0))
     high, low = split_table(back)
     back = jnp.asarray(np.concatenate([high, high, low], axis=0))
-    rounds = 3 + (sizes[0].bit_length() - 1) + (sizes[2].bit_length() - 1)
     exchange = (4, MEMBERS * BLOCK, PTS)
     rim = (MEMBERS, FIELDS, 32, PTS)
     vmem = pltpu.VMEM
@@ -422,8 +450,8 @@
     updated, wall = pl.pallas_call(
         functools.partial(kernel, sizes),
         out_shape=(
-            jax.ShapeDtypeStruct(state.shape, F32),
-            jax.ShapeDtypeStruct((4 * MEMBERS, PTS), F32),
+            pltpu.VMEM(state.shape, F32),
+            pltpu.VMEM((4 * MEMBERS, PTS), F32),
         ),
         in_specs=[pl.BlockSpec(memory_space=pl.ANY)] * 4,
         out_specs=(
@@ -439,8 +467,8 @@
             vmem(back.shape, BF16),
             *[vmem(rim, F32)] * 4,
             *[vmem(exchange, F32)] * 4,
-            vmem((rounds + 1, 16, PTS), F32),
-            vmem((rounds, 16, PTS), F32),
+            vmem((4, 1, PTS), F32),
+            vmem((3, 8, 1, PTS), F32),
             vmem((4 * MEMBERS, PTS), F32),
             vmem((4, 4 * MEMBERS, PTS), F32),
             dma((7,)),
@@ -450,8 +478,8 @@
             dma((4, STEPS)),
             dma((4, GROUPS)),
             dma((4, GROUPS)),
-            dma((rounds,)),
-            dma((rounds,)),
+            dma((3, 7)),
+            dma((3, 8)),
             dma((3,)),
             dma((4,)),
         ],

time: 82.9 us -> 73.7 us (0.89)
  Pallas kernels: 78.1 us -> 71.2 us
  local copies, waits for them, and re-layouts: 3.34 us -> 1.75 us
    pallas_call x1, Pallas kernels: 78.1 us -> 71.2 us  [per_device(): pl.pallas_call(functools.partial(kernel, sizes), out_shape=(pltpu.VMEM(st...]
    unnamed x4 -> x2, local copies, waits for them, and re-layouts: 3.34 us -> 1.75 us
where the time goes in v1:
time: 73.7 us; the launch traced here: 73.6 us
  Pallas kernels  71.2 us (97%)
  local copies, waits for them, and re-layouts  1.75 us (2%)
    pallas_call x1, Pallas kernels, per_device(): pl.pallas_call(functools.partial(kernel, sizes), out_shape=(pltpu.VMEM(st...  71.2 us
    unnamed x2, local copies, waits for them, and re-layouts  1.75 us

profile of v1, /device:TPU:1, one launch (start us, length us, event | category | flops | bytes accessed | tf_op | source)
XLA Modules:
  0.0 73.6 jit_solution(6399169638330485051)
XLA Ops:
  0.6 71.2 %step.1 = (f32[12,4,64,128]{3,2,1,0:T(8,128)S(1)}, f32[48,128]{1,0:T(8,128)S(1)}) custom-call(f32[12,4,64,128]{3,2,1,0:T(8,128)} %state_hbm.1, f32[32,256,256]{2,1,0:T(8,128)} %inverse_hbm.1, bf16[512,256]{1,0:T(8,128)(2,1)} %constant.4.clone.project_hbm, bf16[384,128]{1,0:T(8,128)(2,1)} %constant.5.clone.back_hbm), custom_call_target="tpu_custom_call" | custom-call | tf_op jit(solution)/shard_map/step/pallas_call | solution.py:450
  71.9 1.1 %copy.8 = f32[12,4,64,128]{3,2,1,0:T(8,128)} copy(f32[12,4,64,128]{3,2,1,0:T(8,128)S(1)} %get-tuple-element.6) | data formatting | bytes 3145728
  73.0 0.6 copy.9

commit v2 on v1

--- a/solution.py
+++ b/solution.py
@@ -129,10 +129,25 @@
     stage_size = (nz, nx, 4 * ny)
     peers = [stage_peer(k, n)[1] for k in range(3) for n in range(1, stage_size[k])]
 
+    upper = lax.div(z, nz // 2)
+    depth = upper * (nz - 1 - z) + (1 - upper) * z
+    inner = z + 1 - 2 * upper
+    outer = z - 1 + 2 * upper
+
+    def at_plane(device, plane):
+        return {**device, "gx_2": plane}
+
     barrier = pltpu.get_barrier_semaphore()
     met = [right, left, *peers]
     for device in met:
         pl.semaphore_signal(barrier, inc=1, device_id=device, device_id_type=MESH)
+    for level, plane in ((0, inner), (1, outer)):
+        @pl.when(depth == level)
+        def _():
+            for device in solvers:
+                pl.semaphore_signal(
+                    barrier, inc=1, device_id=at_plane(device, plane), device_id_type=MESH
+                )
 
     state_load = pltpu.make_async_copy(state_hbm, state, local_sem.at[0])
     state_load.start()
@@ -181,8 +196,6 @@
         total = jnp.sum(values * values, axis=0, keepdims=True)
         return jnp.where(lane == e, jnp.sum(total, axis=1, keepdims=True), carry)
 
-    sum_mine[0] = lax.fori_loop(0, MEMBERS, squares, jnp.zeros((1, PTS), F32))
-
     def sum_copies(stage, step):
         index, device = stage_peer(stage, step)
 
@@ -208,10 +221,11 @@
             total = total + sum_all[stage, k]
         sum_mine[stage + 1] = total
 
-    pl.semaphore_wait(barrier, len(met))
-    sum_start(0)
+    pl.semaphore_wait(barrier, len(met) + len(solvers) * (1 - lax.div(depth + 2, 4)))
     for copy in halo_copies(0):
         copy.start()
+    sum_mine[0] = lax.fori_loop(0, MEMBERS, squares, jnp.zeros((1, PTS), F32))
+    sum_start(0)
 
     def pack_and_send(step, carry):
         for k in range(STEP):
@@ -239,12 +253,15 @@
     interior = coefficient < 4 * LOCAL - 2
 
     def mode_copies(step):
+        moved = lax.div(step, STEPS - STEP) * (1 - lax.div(depth + nz - 1, nz))
+        target = step + moved * STEP
         rows = pl.ds(step * (STEP * BLOCK), STEP * BLOCK)
+        target_rows = pl.ds(target * (STEP * BLOCK), STEP * BLOCK)
         return [
             pltpu.make_async_remote_copy(
-                out_modes.at[q, rows], in_modes.at[me, rows],
-                mode_send.at[q, step], mode_recv.at[me, step],
-                device_id=solvers[q], device_id_type=MESH,
+                out_modes.at[q, rows], in_modes.at[me, target_rows],
+                mode_send.at[q, step], mode_recv.at[me, target],
+                device_id=at_plane(solvers[q], z + moved * (1 - 2 * upper)), device_id_type=MESH,
             )
             for q in range(4)
         ]
@@ -294,16 +311,22 @@
 
     lax.fori_loop(0, STEPS, project_step, 0)
 
-    def coef_copies(group):
-        rows = pl.ds(group * (GROUP * BLOCK), GROUP * BLOCK)
+    def coef_copies(slot):
+        moved = lax.div(slot, GROUPS)
+        group = slot - moved
+        rows = pl.ds(slot * (GROUP * BLOCK), GROUP * BLOCK)
+        target_rows = pl.ds(group * (GROUP * BLOCK), GROUP * BLOCK)
         return [
             pltpu.make_async_remote_copy(
-                out_coefs.at[t, rows], in_coefs.at[me, rows],
-                coef_send.at[t, group], coef_recv.at[me, group],
-                device_id=solvers[t], device_id_type=MESH,
+                out_coefs.at[t, rows], in_coefs.at[me, target_rows],
+                coef_send.at[t, slot], coef_recv.at[me, group],
+                device_id=at_plane(solvers[t], z + moved * (2 * upper - 1)), device_id_type=MESH,
             )
             for t in range(4)
         ]
+
+    def solved_here(slot):
+        return (slot < GROUPS - 1) | ((slot == GROUPS - 1) & (depth > 0)) | ((slot == GROUPS) & (depth == 1))
 
     def arrived(buffer, sem, rows, s, k):
         return pltpu.make_async_remote_copy(
@@ -336,7 +359,7 @@
             out_coefs[2 * k, rows, :] = jnp.where(low_half, even[:, lanes], turn(odd[:, lanes]))
             out_coefs[2 * k + 1, rows, :] = jnp.where(low_half, turn(even[:, lanes]), odd[:, lanes])
 
-    def solve_group(group, carry):
+    def solve_group(group):
         for s in range(4):
             for k in range(GROUP // STEP):
                 step = group * (GROUP // STEP) + k
@@ -352,9 +375,15 @@
         lax.fori_loop(0, QUARTER // UNROLL, some_modes, 0)
         for copy in coef_copies(group):
             copy.start()
-        return carry
-
-    lax.fori_loop(0, GROUPS, solve_group, 0)
+
+    def solve_slot(slot, carry):
+        @pl.when(solved_here(slot))
+        def _():
+            solve_group(slot)
+
+        return carry
+
+    lax.fori_loop(0, GROUPS + 1, solve_slot, 0)
 
     row = lax.broadcasted_iota(jnp.int32, (LOCAL, PTS), 0)
     k_float = (me * LOCAL + row).astype(F32)
@@ -424,11 +453,14 @@
     lax.fori_loop(0, STEPS, ended, 0)
 
     def ended_group(group, carry):
-        for copy in coef_copies(group):
-            copy.wait_send()
-        return carry
-
-    lax.fori_loop(0, GROUPS, ended_group, 0)
+        @pl.when(solved_here(group))
+        def _():
+            for copy in coef_copies(group):
+                copy.wait_send()
+
+        return carry
+
+    lax.fori_loop(0, GROUPS + 1, ended_group, 0)
     for stage in range(3):
         for step in range(1, stage_size[stage]):
             sum_copies(stage, step)[0].wait_send()
@@ -444,6 +476,7 @@
     high, low = split_table(back)
     back = jnp.asarray(np.concatenate([high, high, low], axis=0))
     exchange = (4, MEMBERS * BLOCK, PTS)
+    larger = (4, (MEMBERS + GROUP) * BLOCK, PTS)
     rim = (MEMBERS, FIELDS, 32, PTS)
     vmem = pltpu.VMEM
     dma = pltpu.SemaphoreType.DMA
@@ -466,7 +499,10 @@
             vmem(project.shape, BF16),
             vmem(back.shape, BF16),
             *[vmem(rim, F32)] * 4,
-            *[vmem(exchange, F32)] * 4,
+            vmem(exchange, F32),
+            vmem(larger, F32),
+            vmem(larger, F32),
+            vmem(exchange, F32),
             vmem((4, 1, PTS), F32),
             vmem((3, 8, 1, PTS), F32),
             vmem((4 * MEMBERS, PTS), F32),
@@ -475,8 +511,8 @@
             dma((2, STEPS)),
             dma((2, STEPS)),
             dma((4, STEPS)),
-            dma((4, STEPS)),
-            dma((4, GROUPS)),
+            dma((4, STEPS + GROUP // STEP)),
+            dma((4, GROUPS + 1)),
             dma((4, GROUPS)),
             dma((3, 7)),
             dma((3, 8)),

time: 73.7 us -> 70.3 us (0.954)
  Pallas kernels: 71.2 us -> 67.8 us
    pallas_call x1, Pallas kernels: 71.2 us -> 67.8 us  [per_device(): pl.pallas_call(functools.partial(kernel, sizes), out_shape=(pltpu.VMEM(st...]
where the time goes in v2:
time: 70.3 us; the launch traced here: 70.2 us
  Pallas kernels  67.8 us (96%)
  local copies, waits for them, and re-layouts  1.75 us (2%)
    pallas_call x1, Pallas kernels, per_device(): pl.pallas_call(functools.partial(kernel, sizes), out_shape=(pltpu.VMEM(st...  67.8 us
    unnamed x2, local copies, waits for them, and re-layouts  1.75 us

profile of v2, /device:TPU:1, one launch (start us, length us, event | category | flops | bytes accessed | tf_op | source)
XLA Modules:
  0.0 70.2 jit_solution(10874832874135032967)
XLA Ops:
  0.6 67.8 %step.1 = (f32[12,4,64,128]{3,2,1,0:T(8,128)S(1)}, f32[48,128]{1,0:T(8,128)S(1)}) custom-call(f32[12,4,64,128]{3,2,1,0:T(8,128)} %state_hbm.1, f32[32,256,256]{2,1,0:T(8,128)} %inverse_hbm.1, bf16[512,256]{1,0:T(8,128)(2,1)} %constant.4.clone.project_hbm, bf16[384,128]{1,0:T(8,128)(2,1)} %constant.5.clone.back_hbm), custom_call_target="tpu_custom_call" | custom-call | tf_op jit(solution)/shard_map/step/pallas_call | solution.py:483
  68.4 1.1 %copy.8 = f32[12,4,64,128]{3,2,1,0:T(8,128)} copy(f32[12,4,64,128]{3,2,1,0:T(8,128)S(1)} %get-tuple-element.6) | data formatting | bytes 3145728
  69.6 0.6 copy.9

commit v3 on v2

--- a/solution.py
+++ b/solution.py
@@ -81,11 +81,11 @@
 
 def kernel(
     sizes,
-    state_hbm, inverse_hbm, project_hbm, back_hbm, out_ref, wall_ref,
-    state, inverse, inv_high, inv_low, project, back,
+    state_hbm, inverse_hbm, project_hbm, back_hbm, weights_hbm, out_ref, wall_ref,
+    state, inverse, inv_high, inv_low, project, back, weights,
     to_right, to_left, from_left, from_right,
     out_modes, in_modes, out_coefs, in_coefs,
-    sum_mine, sum_all, wall_mine, wall_all,
+    sum_mine, sum_all, wall_out, wall_in,
     local_sem, halo_send, halo_recv, mode_send, mode_recv, coef_send, coef_recv,
     sum_send, sum_recv, wall_send, wall_recv,
 ):
@@ -106,10 +106,6 @@
     right = place(lax.rem(here + 1, count))
     left = place(lax.rem(here + count - 1, count))
     solvers = [{"gx_1": 1 - y, "gy_0": q // 2, "gy_1": q % 2} for q in range(4)]
-
-    def other(step):
-        index = lax.rem(me + step, 4)
-        return index, {"gy_0": lax.div(index, 2), "gy_1": lax.rem(index, 2)}
 
     def stage_peer(stage, step):
         if stage == 0:
@@ -154,6 +150,7 @@
     loads = [
         pltpu.make_async_copy(project_hbm, project, local_sem.at[1]),
         pltpu.make_async_copy(back_hbm, back, local_sem.at[2]),
+        pltpu.make_async_copy(weights_hbm, weights, local_sem.at[7]),
     ]
     for k in range(4):
         part = pl.ds(k * 8, 8)
@@ -311,19 +308,49 @@
 
     lax.fori_loop(0, STEPS, project_step, 0)
 
-    def coef_copies(slot):
+    def back_to(slot, t):
+        return at_plane(solvers[t], z + lax.div(slot, GROUPS) * (2 * upper - 1))
+
+    def coef_copies(step):
+        slot = lax.div(step, GROUP // STEP)
         moved = lax.div(slot, GROUPS)
-        group = slot - moved
-        rows = pl.ds(slot * (GROUP * BLOCK), GROUP * BLOCK)
-        target_rows = pl.ds(group * (GROUP * BLOCK), GROUP * BLOCK)
+        target = step - moved * (GROUP // STEP)
+        rows = pl.ds(step * (STEP * BLOCK), STEP * BLOCK)
+        target_rows = pl.ds(target * (STEP * BLOCK), STEP * BLOCK)
         return [
             pltpu.make_async_remote_copy(
                 out_coefs.at[t, rows], in_coefs.at[me, target_rows],
-                coef_send.at[t, slot], coef_recv.at[me, group],
-                device_id=at_plane(solvers[t], z + moved * (2 * upper - 1)), device_id_type=MESH,
+                coef_send.at[t, step], coef_recv.at[me, target],
+                device_id=back_to(slot, t), device_id_type=MESH,
             )
             for t in range(4)
         ]
+
+    def wall_copies(slot):
+        group = slot - lax.div(slot, GROUPS)
+        return [
+            pltpu.make_async_remote_copy(
+                wall_out.at[slot], wall_in.at[me, group],
+                wall_send.at[t, slot], wall_recv.at[me, group],
+                device_id=back_to(slot, t), device_id_type=MESH,
+            )
+            for t in range(4)
+        ]
+
+    def wall_arrived(q, group):
+        return pltpu.make_async_remote_copy(
+            wall_in.at[q, group], wall_in.at[q, group],
+            wall_recv.at[q, group], wall_recv.at[q, group],
+            device_id=solvers[q], device_id_type=MESH,
+        )
+
+    def wall_sums(slot):
+        rows = pl.ds(slot * (GROUP * BLOCK), GROUP * BLOCK)
+        blocks = jnp.concatenate([out_coefs[t, rows, :] for t in range(4)], axis=1)
+        high, low = split(blocks)
+        first = dot_t(weights[...], high)
+        second = dot_t(weights[:16], low)
+        wall_out[slot] = (first[:16] + (first[16:] + second))[:2]
 
     def solved_here(slot):
         return (slot < GROUPS - 1) | ((slot == GROUPS - 1) & (depth > 0)) | ((slot == GROUPS) & (depth == 1))
@@ -373,7 +400,11 @@
             return carry
 
         lax.fori_loop(0, QUARTER // UNROLL, some_modes, 0)
-        for copy in coef_copies(group):
+        for k in range(GROUP // STEP):
+            for copy in coef_copies(group * (GROUP // STEP) + k):
+                copy.start()
+        wall_sums(group)
+        for copy in wall_copies(group):
             copy.start()
 
     def solve_slot(slot, carry):
@@ -385,10 +416,6 @@
 
     lax.fori_loop(0, GROUPS + 1, solve_slot, 0)
 
-    row = lax.broadcasted_iota(jnp.int32, (LOCAL, PTS), 0)
-    k_float = (me * LOCAL + row).astype(F32)
-    curvature = k_float * k_float / float((4 * LOCAL) ** 2)
-    parity = jnp.where(lax.rem(row[:8], 2) == 0, -1.0, 1.0)
     grid = float(FIELDS * 4 * LOCAL * PTS * count)
 
     sum_end(2)
@@ -403,45 +430,46 @@
             turned.append(block.T)
         high, low = split(jnp.concatenate(turned, axis=0))
         values = dot(jnp.concatenate([high, low], axis=1), back[: 2 * MODES])
-        values = values + dot(high, back[2 * MODES :])
+        values = values + dot(high, back[2 * MODES : 3 * MODES])
         total = jnp.sum(jnp.where(lane == e, sum_mine[3], 0.0), axis=1, keepdims=True)
         values = values * lax.rsqrt(total / grid + EPSILON)
         out_ref[e] = values.reshape(FIELDS, LOCAL, PTS)
-        for c in range(2):
-            weighted = values[c * PTS : c * PTS + LOCAL] * curvature
-            rows = jnp.sum(weighted.reshape(LOCAL // 8, 8, PTS), axis=0)
-            wall_mine[pl.ds(e * 4 + c, 1), :] = jnp.sum(rows, axis=0, keepdims=True)
-            wall_mine[pl.ds(e * 4 + 2 + c, 1), :] = jnp.sum(rows * parity, axis=0, keepdims=True)
-
-    def back_group(group, carry):
-        rows = pl.ds(group * (GROUP * BLOCK), GROUP * BLOCK)
+
+    row = lax.broadcasted_iota(jnp.int32, (4 * GROUP, 2 * PTS), 0)
+    lanes = lax.broadcasted_iota(jnp.int32, (4 * GROUP, 2 * PTS), 1)
+    own = lax.div(lanes, QUARTER) == 2 * lax.div(row, 4) + lax.rem(row, 2)
+    upper_wall = lax.rem(lax.div(row, 2), 2) == 0
+
+    def wall_group(group):
+        parts = []
+        for q in range(4):
+            wall_arrived(q, group).wait_recv()
+            both = wall_in[q, group]
+            parts.append(jnp.where(own, jnp.where(upper_wall, both[:1], both[1:]), 0.0))
+        high, low = split(jnp.concatenate(parts, axis=1))
+        table = back[3 * MODES : 11 * MODES]
+        first = dot(jnp.concatenate([high, low], axis=0), table)
+        count = 4 * GROUP
+        values = first[:count] + (first[count:] + dot(high, back[11 * MODES :]))
+        member = group * GROUP + lax.div(row[:, :PTS], 4)
+        total = jnp.sum(jnp.where(lane == member, sum_mine[3], 0.0), axis=1, keepdims=True)
+        values = values * lax.rsqrt(total / grid + EPSILON)
+        wall_ref[pl.ds(pl.multiple_of(group * count, count), count), :] = values
+
+    def back_step(step, carry):
+        rows = pl.ds(step * (STEP * BLOCK), STEP * BLOCK)
         for s in range(4):
-            arrived(in_coefs, coef_recv, rows, s, group).wait_recv()
-
-        def one(k, carry):
-            back_member(group * GROUP + k)
-            return carry
-
-        lax.fori_loop(0, GROUP, one, 0)
-        return carry
-
-    lax.fori_loop(0, GROUPS, back_group, 0)
-
-    def wall_copy(step):
-        index, device = other(step)
-        send = pltpu.make_async_remote_copy(
-            wall_mine, wall_all.at[me], wall_send.at[step - 1], wall_recv.at[me],
-            device_id=device, device_id_type=MESH,
-        )
-        receive = pltpu.make_async_remote_copy(
-            wall_mine, wall_all.at[index], wall_send.at[step - 1], wall_recv.at[index],
-            device_id=device, device_id_type=MESH,
-        )
-        return send, receive
-
-    for step in (1, 2, 3):
-        wall_copy(step)[0].start()
-    wall_all[me] = wall_mine[...]
+            arrived(in_coefs, coef_recv, rows, s, step).wait_recv()
+        for k in range(STEP):
+            back_member(step * STEP + k)
+
+        @pl.when(lax.rem(step, 2) == 1)
+        def _():
+            wall_group(lax.div(step, 2))
+
+        return carry
+
+    lax.fori_loop(0, STEPS, back_step, 0)
 
     def ended(step, carry):
         for copy in halo_copies(step):
@@ -455,7 +483,10 @@
     def ended_group(group, carry):
         @pl.when(solved_here(group))
         def _():
-            for copy in coef_copies(group):
+            for k in range(GROUP // STEP):
+                for copy in coef_copies(group * (GROUP // STEP) + k):
+                    copy.wait_send()
+            for copy in wall_copies(group):
                 copy.wait_send()
 
         return carry
@@ -464,17 +495,24 @@
     for stage in range(3):
         for step in range(1, stage_size[stage]):
             sum_copies(stage, step)[0].wait_send()
-    for step in (1, 2, 3):
-        wall_copy(step)[0].wait_send()
-        wall_copy(step)[1].wait_recv()
-    wall_ref[...] = (wall_all[0] + wall_all[1]) + (wall_all[2] + wall_all[3])
 
 
 def per_device(sizes, state, inverse):
     both, back = window_tables(PTS + 2 * HALO, HALO, PTS, MODES)
     project = jnp.asarray(np.concatenate(split_table(both), axis=0))
     high, low = split_table(back)
-    back = jnp.asarray(np.concatenate([high, high, low], axis=0))
+
+    def tiled(table):
+        quarters = table.reshape(4, QUARTER, PTS)
+        return np.concatenate([q for part in quarters for q in [part] * (2 * GROUP)], axis=0)
+
+    back = jnp.asarray(np.concatenate([high, high, low, tiled(high), tiled(low)], axis=0))
+    k = np.arange(4 * LOCAL, dtype=np.float64)
+    curvature = k * k / (4 * LOCAL) ** 2
+    walls = np.zeros((16, 4, 2, LOCAL))
+    walls[0, :, 0] = curvature.reshape(4, LOCAL)
+    walls[1, :, 0] = np.where(k % 2 == 0, -curvature, curvature).reshape(4, LOCAL)
+    weights = jnp.asarray(np.concatenate(split_table(walls.reshape(16, 8 * LOCAL)), axis=0))
     exchange = (4, MEMBERS * BLOCK, PTS)
     larger = (4, (MEMBERS + GROUP) * BLOCK, PTS)
     rim = (MEMBERS, FIELDS, 32, PTS)
@@ -486,7 +524,7 @@
             pltpu.VMEM(state.shape, F32),
             pltpu.VMEM((4 * MEMBERS, PTS), F32),
         ),
-        in_specs=[pl.BlockSpec(memory_space=pl.ANY)] * 4,
+        in_specs=[pl.BlockSpec(memory_space=pl.ANY)] * 5,
         out_specs=(
             pl.BlockSpec(memory_space=pltpu.VMEM),
             pl.BlockSpec(memory_space=pltpu.VMEM),
@@ -498,6 +536,7 @@
             vmem(inverse.shape, BF16),
             vmem(project.shape, BF16),
             vmem(back.shape, BF16),
+            vmem(weights.shape, BF16),
             *[vmem(rim, F32)] * 4,
             vmem(exchange, F32),
             vmem(larger, F32),
@@ -505,25 +544,25 @@
             vmem(exchange, F32),
             vmem((4, 1, PTS), F32),
             vmem((3, 8, 1, PTS), F32),
-            vmem((4 * MEMBERS, PTS), F32),
-            vmem((4, 4 * MEMBERS, PTS), F32),
-            dma((7,)),
+            vmem((GROUPS + 1, 2, 2 * PTS), F32),
+            vmem((4, GROUPS, 2, 2 * PTS), F32),
+            dma((8,)),
             dma((2, STEPS)),
             dma((2, STEPS)),
             dma((4, STEPS)),
             dma((4, STEPS + GROUP // STEP)),
+            dma((4, STEPS + GROUP // STEP)),
+            dma((4, STEPS)),
+            dma((3, 7)),
+            dma((3, 8)),
             dma((4, GROUPS + 1)),
             dma((4, GROUPS)),
-            dma((3, 7)),
-            dma((3, 8)),
-            dma((3,)),
-            dma((4,)),
         ],
         compiler_params=pltpu.CompilerParams(
             collective_id=0, has_side_effects=True, vmem_limit_bytes=56 * 1024 * 1024
         ),
         name="step",
-    )(state, inverse, project, back)
+    )(state, inverse, project, back, weights)
     return updated, wall.reshape(MEMBERS, 2, 2, PTS)
 
 

time: 70.3 us -> 66.9 us (0.952)
  Pallas kernels: 67.8 us -> 64.4 us
    pallas_call x1, Pallas kernels: 67.8 us -> 64.4 us  [per_device(): pl.pallas_call(functools.partial(kernel, sizes), out_shape=(pltpu.VMEM(st...]
where the time goes in v3:
time: 66.9 us; the launch traced here: 66.8 us
  Pallas kernels  64.4 us (96%)
  local copies, waits for them, and re-layouts  1.75 us (3%)
    pallas_call x1, Pallas kernels, per_device(): pl.pallas_call(functools.partial(kernel, sizes), out_shape=(pltpu.VMEM(st...  64.4 us
    unnamed x2, local copies, waits for them, and re-layouts  1.75 us

profile of v3, /device:TPU:1, one launch (start us, length us, event | category | flops | bytes accessed | tf_op | source)
XLA Modules:
  0.0 66.8 jit_solution(18277464625777625785)
XLA Ops:
  0.6 64.4 %step.1 = (f32[12,4,64,128]{3,2,1,0:T(8,128)S(1)}, f32[48,128]{1,0:T(8,128)S(1)}) custom-call(f32[12,4,64,128]{3,2,1,0:T(8,128)} %state_hbm.1, f32[32,256,256]{2,1,0:T(8,128)} %inverse_hbm.1, bf16[512,256]{1,0:T(8,128)(2,1)} %constant.6.clone.project_hbm, bf16[2432,128]{1,0:T(8,128)(2,1)} %constant.7.clone.back_hbm, bf16[32,512]{1,0:T(8,128)(2,1)} %constant.8.clone.weights_hbm), custom_call_target="tpu_custom_call" | custom-call | tf_op jit(solution)/shard_map/step/pallas_call | solution.py:521
  65.0 1.1 %copy.9 = f32[12,4,64,128]{3,2,1,0:T(8,128)} copy(f32[12,4,64,128]{3,2,1,0:T(8,128)S(1)} %get-tuple-element.6) | data formatting | bytes 3145728
  66.2 0.6 copy.10

commit v4 on v3

--- a/solution.py
+++ b/solution.py
@@ -34,6 +34,7 @@
 GROUP = 4
 GROUPS = MEMBERS // GROUP
 UNROLL = 8
+PIECES = QUARTER // UNROLL
 
 
 def window_tables(window, rim, points, modes):
@@ -83,11 +84,11 @@
     sizes,
     state_hbm, inverse_hbm, project_hbm, back_hbm, weights_hbm, out_ref, wall_ref,
     state, inverse, inv_high, inv_low, project, back, weights,
-    to_right, to_left, from_left, from_right,
+    sides, rims,
     out_modes, in_modes, out_coefs, in_coefs,
     sum_mine, sum_all, wall_out, wall_in,
     local_sem, halo_send, halo_recv, mode_send, mode_recv, coef_send, coef_recv,
-    sum_send, sum_recv, wall_send, wall_recv,
+    sum_send, sum_recv, wall_recv,
 ):
     nx, ny, nz = sizes
     x, y, z = (lax.axis_index(a) for a in GX)
@@ -145,45 +146,49 @@
                     barrier, inc=1, device_id=at_plane(device, plane), device_id_type=MESH
                 )
 
-    state_load = pltpu.make_async_copy(state_hbm, state, local_sem.at[0])
-    state_load.start()
+    state_loads = []
+    for part, sem in ((pl.ds(0, STEP), 0), (pl.ds(STEP, MEMBERS - STEP), 8)):
+        state_loads.append(
+            pltpu.make_async_copy(state_hbm.at[part], state.at[part], local_sem.at[sem])
+        )
+    for load in state_loads:
+        load.start()
     loads = [
         pltpu.make_async_copy(project_hbm, project, local_sem.at[1]),
         pltpu.make_async_copy(back_hbm, back, local_sem.at[2]),
         pltpu.make_async_copy(weights_hbm, weights, local_sem.at[7]),
     ]
-    for k in range(4):
-        part = pl.ds(k * 8, 8)
-        loads.append(
-            pltpu.make_async_copy(inverse_hbm.at[part], inverse.at[part], local_sem.at[3 + k])
-        )
+
+    def inverse_load(k):
+        part = pl.ds(k * UNROLL, UNROLL)
+        return pltpu.make_async_copy(inverse_hbm.at[part], inverse.at[part], local_sem.at[3 + k])
 
     lane = lax.broadcasted_iota(jnp.int32, (1, PTS), 1)
     low_half = lane < LOCAL
 
     def halo_copies(step):
         rows = pl.ds(step * STEP, STEP)
-        return (
+        return [
             pltpu.make_async_remote_copy(
-                to_right.at[rows], from_left.at[rows], halo_send.at[0, step], halo_recv.at[0, step],
-                device_id=right, device_id_type=MESH,
-            ),
-            pltpu.make_async_remote_copy(
-                to_left.at[rows], from_right.at[rows], halo_send.at[1, step], halo_recv.at[1, step],
-                device_id=left, device_id_type=MESH,
-            ),
+                sides.at[k, rows], rims.at[k, rows], halo_send.at[0], halo_recv.at[step],
+                device_id=device, device_id_type=MESH,
+            )
+            for k, device in enumerate((right, left))
+        ]
+
+    def whole(buffer, sem):
+        return pltpu.make_async_remote_copy(
+            buffer, buffer, sem, sem, device_id=right, device_id_type=MESH
         )
 
-    state_load.wait()
-    for load in loads:
-        load.start()
+    state_loads[0].wait()
 
     def pack(e):
         centre = state[e]
         top, low = centre[:, :32], centre[:, 32:]
         turned = pltpu.roll(low, LOCAL, 2)
-        to_right[e] = jnp.where(low_half, turned, top)
-        to_left[e] = jnp.where(low_half, top, turned)
+        sides[0, e] = jnp.where(low_half, turned, top)
+        sides[1, e] = jnp.where(low_half, top, turned)
 
     for k in range(STEP):
         pack(k)
@@ -193,26 +198,23 @@
         total = jnp.sum(values * values, axis=0, keepdims=True)
         return jnp.where(lane == e, jnp.sum(total, axis=1, keepdims=True), carry)
 
-    def sum_copies(stage, step):
-        index, device = stage_peer(stage, step)
-
-        def copy(slot):
-            return pltpu.make_async_remote_copy(
-                sum_mine.at[stage], sum_all.at[stage, slot],
-                sum_send.at[stage, step - 1], sum_recv.at[stage, slot],
-                device_id=device, device_id_type=MESH,
-            )
-
-        return copy(stage_me[stage]), copy(index)
+    def sum_copy(stage, step):
+        return pltpu.make_async_remote_copy(
+            sum_mine.at[stage], sum_all.at[stage, stage_me[stage]],
+            sum_send.at[stage], sum_recv.at[stage],
+            device_id=stage_peer(stage, step)[1], device_id_type=MESH,
+        )
+
+    def sum_rest(stage, sem):
+        return whole(sum_all.at[stage, pl.ds(0, stage_size[stage] - 1)], sem.at[stage])
 
     def sum_start(stage):
         for step in range(1, stage_size[stage]):
-            sum_copies(stage, step)[0].start()
+            sum_copy(stage, step).start()
         sum_all[stage, stage_me[stage]] = sum_mine[stage]
 
     def sum_end(stage):
-        for step in range(1, stage_size[stage]):
-            sum_copies(stage, step)[1].wait_recv()
+        sum_rest(stage, sum_recv).wait_recv()
         total = sum_all[stage, 0]
         for k in range(1, stage_size[stage]):
             total = total + sum_all[stage, k]
@@ -221,6 +223,11 @@
     pl.semaphore_wait(barrier, len(met) + len(solvers) * (1 - lax.div(depth + 2, 4)))
     for copy in halo_copies(0):
         copy.start()
+    state_loads[1].wait()
+    for load in loads:
+        load.start()
+    for k in range(PIECES):
+        inverse_load(k).start()
     sum_mine[0] = lax.fori_loop(0, MEMBERS, squares, jnp.zeros((1, PTS), F32))
     sum_start(0)
 
@@ -242,7 +249,6 @@
         inv_low[m] = low
         return carry
 
-    lax.fori_loop(0, QUARTER, split_inverse, 0)
 
     coupling_0 = jnp.where(low_half, TIME_STEP * CORIOLIS, TIME_STEP)
     coupling_1 = jnp.where(low_half, -TIME_STEP * CORIOLIS, -TIME_STEP * STRATIFICATION)
@@ -257,7 +263,7 @@
         return [
             pltpu.make_async_remote_copy(
                 out_modes.at[q, rows], in_modes.at[me, target_rows],
-                mode_send.at[q, step], mode_recv.at[me, target],
+                mode_send.at[0], mode_recv.at[lax.div(target, GROUP // STEP)],
                 device_id=at_plane(solvers[q], z + moved * (1 - 2 * upper)), device_id_type=MESH,
             )
             for q in range(4)
@@ -265,7 +271,7 @@
 
     def project_member(e):
         centre = state[e]
-        rim_left, rim_right = from_left[e], from_right[e]
+        rim_left, rim_right = rims[0, e], rims[1, e]
         top = jnp.where(low_half, rim_right, rim_left)
         low = pltpu.roll(jnp.where(low_half, rim_left, rim_right), LOCAL, 2)
         rim = jnp.concatenate([top, low], axis=1)
@@ -287,12 +293,16 @@
             out_modes[q, pl.ds(base + QUARTER, QUARTER), :] = rhs_1[modes]
 
     def project_step(step, carry):
-        for copy in halo_copies(step):
-            copy.wait_recv()
+        whole(rims.at[:, pl.ds(step * STEP, STEP)], halo_recv.at[step]).wait_recv()
         for k in range(STEP):
             project_member(step * STEP + k)
         for copy in mode_copies(step):
             copy.start()
+
+        @pl.when(step < PIECES)
+        def _():
+            inverse_load(step).wait()
+            lax.fori_loop(step * UNROLL, (step + 1) * UNROLL, split_inverse, 0)
 
         @pl.when(step == 2)
         def _():
@@ -320,7 +330,7 @@
         return [
             pltpu.make_async_remote_copy(
                 out_coefs.at[t, rows], in_coefs.at[me, target_rows],
-                coef_send.at[t, step], coef_recv.at[me, target],
+                coef_send.at[0], coef_recv.at[target],
                 device_id=back_to(slot, t), device_id_type=MESH,
             )
             for t in range(4)
@@ -331,18 +341,11 @@
         return [
             pltpu.make_async_remote_copy(
                 wall_out.at[slot], wall_in.at[me, group],
-                wall_send.at[t, slot], wall_recv.at[me, group],
+                coef_send.at[1], wall_recv.at[group],
                 device_id=back_to(slot, t), device_id_type=MESH,
             )
             for t in range(4)
         ]
-
-    def wall_arrived(q, group):
-        return pltpu.make_async_remote_copy(
-            wall_in.at[q, group], wall_in.at[q, group],
-            wall_recv.at[q, group], wall_recv.at[q, group],
-            device_id=solvers[q], device_id_type=MESH,
-        )
 
     def wall_sums(slot):
         rows = pl.ds(slot * (GROUP * BLOCK), GROUP * BLOCK)
@@ -354,12 +357,6 @@
 
     def solved_here(slot):
         return (slot < GROUPS - 1) | ((slot == GROUPS - 1) & (depth > 0)) | ((slot == GROUPS) & (depth == 1))
-
-    def arrived(buffer, sem, rows, s, k):
-        return pltpu.make_async_remote_copy(
-            buffer.at[s, rows], buffer.at[s, rows], sem.at[s, k], sem.at[s, k],
-            device_id=solvers[s], device_id_type=MESH,
-        )
 
     def turn(a):
         return pltpu.roll(a, LOCAL, 1)
@@ -387,11 +384,8 @@
             out_coefs[2 * k + 1, rows, :] = jnp.where(low_half, turn(even[:, lanes]), odd[:, lanes])
 
     def solve_group(group):
-        for s in range(4):
-            for k in range(GROUP // STEP):
-                step = group * (GROUP // STEP) + k
-                rows = pl.ds(step * (STEP * BLOCK), STEP * BLOCK)
-                arrived(in_modes, mode_recv, rows, s, step).wait_recv()
+        rows = pl.ds(group * (GROUP * BLOCK), GROUP * BLOCK)
+        whole(in_modes.at[:, rows], mode_recv.at[group]).wait_recv()
         base = group * (GROUP * BLOCK)
 
         def some_modes(k, carry):
@@ -407,7 +401,9 @@
         for copy in wall_copies(group):
             copy.start()
 
-    def solve_slot(slot, carry):
+    def solve_slot(turn, carry):
+        slot = turn + lax.div(turn, GROUPS - 1) * (1 - 2 * lax.rem(turn, GROUPS - 1))
+
         @pl.when(solved_here(slot))
         def _():
             solve_group(slot)
@@ -415,6 +411,11 @@
         return carry
 
     lax.fori_loop(0, GROUPS + 1, solve_slot, 0)
+
+    whole(sides, halo_send.at[0]).wait_send()
+    whole(out_modes, mode_send.at[0]).wait_send()
+    for stage in range(3):
+        sum_rest(stage, sum_send).wait_send()
 
     grid = float(FIELDS * 4 * LOCAL * PTS * count)
 
@@ -441,9 +442,9 @@
     upper_wall = lax.rem(lax.div(row, 2), 2) == 0
 
     def wall_group(group):
+        whole(wall_in.at[:, group], wall_recv.at[group]).wait_recv()
         parts = []
         for q in range(4):
-            wall_arrived(q, group).wait_recv()
             both = wall_in[q, group]
             parts.append(jnp.where(own, jnp.where(upper_wall, both[:1], both[1:]), 0.0))
         high, low = split(jnp.concatenate(parts, axis=1))
@@ -454,12 +455,13 @@
         member = group * GROUP + lax.div(row[:, :PTS], 4)
         total = jnp.sum(jnp.where(lane == member, sum_mine[3], 0.0), axis=1, keepdims=True)
         values = values * lax.rsqrt(total / grid + EPSILON)
-        wall_ref[pl.ds(pl.multiple_of(group * count, count), count), :] = values
+        for e in range(GROUP):
+            for w in range(2):
+                wall_ref[group * GROUP + e, w] = values[4 * e + 2 * w : 4 * e + 2 * w + 2]
 
     def back_step(step, carry):
         rows = pl.ds(step * (STEP * BLOCK), STEP * BLOCK)
-        for s in range(4):
-            arrived(in_coefs, coef_recv, rows, s, step).wait_recv()
+        whole(in_coefs.at[:, rows], coef_recv.at[step]).wait_recv()
         for k in range(STEP):
             back_member(step * STEP + k)
 
@@ -471,30 +473,13 @@
 
     lax.fori_loop(0, STEPS, back_step, 0)
 
-    def ended(step, carry):
-        for copy in halo_copies(step):
-            copy.wait_send()
-        for copy in mode_copies(step):
-            copy.wait_send()
-        return carry
-
-    lax.fori_loop(0, STEPS, ended, 0)
-
-    def ended_group(group, carry):
-        @pl.when(solved_here(group))
-        def _():
-            for k in range(GROUP // STEP):
-                for copy in coef_copies(group * (GROUP // STEP) + k):
-                    copy.wait_send()
-            for copy in wall_copies(group):
-                copy.wait_send()
-
-        return carry
-
-    lax.fori_loop(0, GROUPS + 1, ended_group, 0)
-    for stage in range(3):
-        for step in range(1, stage_size[stage]):
-            sum_copies(stage, step)[0].wait_send()
+    for held, here_now in (
+        (GROUPS - 1, depth == 0), (GROUPS + 1, depth == 1), (GROUPS, depth > 1)
+    ):
+        @pl.when(here_now)
+        def _():
+            whole(out_coefs.at[:, pl.ds(0, held * GROUP * BLOCK)], coef_send.at[0]).wait_send()
+            whole(wall_in.at[:, pl.ds(0, held)], coef_send.at[1]).wait_send()
 
 
 def per_device(sizes, state, inverse):
@@ -515,14 +500,14 @@
     weights = jnp.asarray(np.concatenate(split_table(walls.reshape(16, 8 * LOCAL)), axis=0))
     exchange = (4, MEMBERS * BLOCK, PTS)
     larger = (4, (MEMBERS + GROUP) * BLOCK, PTS)
-    rim = (MEMBERS, FIELDS, 32, PTS)
+    rim = (2, MEMBERS, FIELDS, 32, PTS)
     vmem = pltpu.VMEM
     dma = pltpu.SemaphoreType.DMA
     updated, wall = pl.pallas_call(
         functools.partial(kernel, sizes),
         out_shape=(
             pltpu.VMEM(state.shape, F32),
-            pltpu.VMEM((4 * MEMBERS, PTS), F32),
+            pltpu.VMEM((MEMBERS, 2, 2, PTS), F32),
         ),
         in_specs=[pl.BlockSpec(memory_space=pl.ANY)] * 5,
         out_specs=(
@@ -537,7 +522,7 @@
             vmem(project.shape, BF16),
             vmem(back.shape, BF16),
             vmem(weights.shape, BF16),
-            *[vmem(rim, F32)] * 4,
+            *[vmem(rim, F32)] * 2,
             vmem(exchange, F32),
             vmem(larger, F32),
             vmem(larger, F32),
@@ -545,25 +530,24 @@
             vmem((4, 1, PTS), F32),
             vmem((3, 8, 1, PTS), F32),
             vmem((GROUPS + 1, 2, 2 * PTS), F32),
-            vmem((4, GROUPS, 2, 2 * PTS), F32),
-            dma((8,)),
-            dma((2, STEPS)),
-            dma((2, STEPS)),
-            dma((4, STEPS)),
-            dma((4, STEPS + GROUP // STEP)),
-            dma((4, STEPS + GROUP // STEP)),
-            dma((4, STEPS)),
-            dma((3, 7)),
-            dma((3, 8)),
-            dma((4, GROUPS + 1)),
-            dma((4, GROUPS)),
+            vmem((4, GROUPS + 1, 2, 2 * PTS), F32),
+            dma((9,)),
+            dma((1,)),
+            dma((STEPS,)),
+            dma((1,)),
+            dma((GROUPS + 1,)),
+            dma((2,)),
+            dma((STEPS,)),
+            dma((3,)),
+            dma((3,)),
+            dma((GROUPS,)),
         ],
         compiler_params=pltpu.CompilerParams(
             collective_id=0, has_side_effects=True, vmem_limit_bytes=56 * 1024 * 1024
         ),
         name="step",
     )(state, inverse, project, back, weights)
-    return updated, wall.reshape(MEMBERS, 2, 2, PTS)
+    return updated, wall
 
 
 def solution(mesh):

time: 66.9 us -> 63.4 us (0.948)
  Pallas kernels: 64.4 us -> 60.9 us
    pallas_call x1, Pallas kernels: 64.4 us -> 60.9 us  [per_device(): pl.pallas_call(functools.partial(kernel, sizes), out_shape=(pltpu.VMEM(st...]
where the time goes in v4:
time: 63.4 us; the launch traced here: 63.3 us
  Pallas kernels  60.9 us (96%)
  local copies, waits for them, and re-layouts  1.75 us (3%)
  between operations  0.64 us (1%)
    pallas_call x1, Pallas kernels, per_device(): pl.pallas_call(functools.partial(kernel, sizes), out_shape=(pltpu.VMEM(st...  60.9 us
    unnamed x2, local copies, waits for them, and re-layouts  1.75 us

profile of v4, /device:TPU:1, one launch (start us, length us, event | category | flops | bytes accessed | tf_op | source)
XLA Modules:
  0.0 63.3 jit_solution(7645903613239851305)
XLA Ops:
  0.6 60.9 %step.1 = (f32[12,4,64,128]{3,2,1,0:T(8,128)S(1)}, f32[12,2,2,128]{3,2,1,0:T(2,128)S(1)}) custom-call(f32[12,4,64,128]{3,2,1,0:T(8,128)} %state_hbm.1, f32[32,256,256]{2,1,0:T(8,128)} %inverse_hbm.1, bf16[512,256]{1,0:T(8,128)(2,1)} %constant.6.clone.project_hbm, bf16[2432,128]{1,0:T(8,128)(2,1)} %constant.7.clone.back_hbm, ...), custom_call_target="tpu_custom_call" | custom-call | tf_op jit(solution)/shard_map/step/pallas_call | solution.py:506
  61.6 1.1 %copy.9 = f32[12,4,64,128]{3,2,1,0:T(8,128)} copy(f32[12,4,64,128]{3,2,1,0:T(8,128)S(1)} %get-tuple-element.2) | data formatting | bytes 3145728
  62.7 0.6 copy.10

commit v5 on v4

--- a/solution.py
+++ b/solution.py
@@ -31,10 +31,15 @@
 BLOCK = 2 * QUARTER
 STEP = 2
 STEPS = MEMBERS // STEP
-GROUP = 4
+GROUP = 2
 GROUPS = MEMBERS // GROUP
-UNROLL = 8
-PIECES = QUARTER // UNROLL
+UNROLL = 32
+SPAN = 2 * GROUP * QUARTER
+MOVED = (3, 1)
+FOREIGN = 3
+SLOTS = GROUPS + FOREIGN
+PIECES = 4
+PIECE = QUARTER // PIECES
 
 
 def window_tables(window, rim, points, modes):
@@ -128,6 +133,12 @@
 
     upper = lax.div(z, nz // 2)
     depth = upper * (nz - 1 - z) + (1 - upper) * z
+    from_top = nz // 2 - 1 - depth
+    at_0 = lax.div(from_top, 3)
+    at_1 = lax.div(from_top, 2) - at_0
+    at_2 = from_top - 2 * lax.div(from_top, 2) - at_0
+    leaving = MOVED[0] * at_0 + MOVED[1] * at_1
+    coming = MOVED[0] * at_1 + MOVED[1] * at_2
     inner = z + 1 - 2 * upper
     outer = z - 1 + 2 * upper
 
@@ -138,8 +149,8 @@
     met = [right, left, *peers]
     for device in met:
         pl.semaphore_signal(barrier, inc=1, device_id=device, device_id_type=MESH)
-    for level, plane in ((0, inner), (1, outer)):
-        @pl.when(depth == level)
+    for near_end, plane in ((depth < 2, inner), ((depth == 1) | (depth == 2), outer)):
+        @pl.when(near_end)
         def _():
             for device in solvers:
                 pl.semaphore_signal(
@@ -160,7 +171,7 @@
     ]
 
     def inverse_load(k):
-        part = pl.ds(k * UNROLL, UNROLL)
+        part = pl.ds(k * PIECE, PIECE)
         return pltpu.make_async_copy(inverse_hbm.at[part], inverse.at[part], local_sem.at[3 + k])
 
     lane = lax.broadcasted_iota(jnp.int32, (1, PTS), 1)
@@ -220,7 +231,7 @@
             total = total + sum_all[stage, k]
         sum_mine[stage + 1] = total
 
-    pl.semaphore_wait(barrier, len(met) + len(solvers) * (1 - lax.div(depth + 2, 4)))
+    pl.semaphore_wait(barrier, len(met) + len(solvers) * (at_0 + 2 * at_1 + at_2))
     for copy in halo_copies(0):
         copy.start()
     state_loads[1].wait()
@@ -256,14 +267,14 @@
     interior = coefficient < 4 * LOCAL - 2
 
     def mode_copies(step):
-        moved = lax.div(step, STEPS - STEP) * (1 - lax.div(depth + nz - 1, nz))
-        target = step + moved * STEP
+        moved = lax.div(step + leaving, GROUPS)
+        target = step + moved * FOREIGN
         rows = pl.ds(step * (STEP * BLOCK), STEP * BLOCK)
         target_rows = pl.ds(target * (STEP * BLOCK), STEP * BLOCK)
         return [
             pltpu.make_async_remote_copy(
                 out_modes.at[q, rows], in_modes.at[me, target_rows],
-                mode_send.at[0], mode_recv.at[lax.div(target, GROUP // STEP)],
+                mode_send.at[0], mode_recv.at[target],
                 device_id=at_plane(solvers[q], z + moved * (1 - 2 * upper)), device_id_type=MESH,
             )
             for q in range(4)
@@ -302,7 +313,7 @@
         @pl.when(step < PIECES)
         def _():
             inverse_load(step).wait()
-            lax.fori_loop(step * UNROLL, (step + 1) * UNROLL, split_inverse, 0)
+            lax.fori_loop(step * PIECE, (step + 1) * PIECE, split_inverse, 0)
 
         @pl.when(step == 2)
         def _():
@@ -321,11 +332,9 @@
     def back_to(slot, t):
         return at_plane(solvers[t], z + lax.div(slot, GROUPS) * (2 * upper - 1))
 
-    def coef_copies(step):
-        slot = lax.div(step, GROUP // STEP)
-        moved = lax.div(slot, GROUPS)
-        target = step - moved * (GROUP // STEP)
-        rows = pl.ds(step * (STEP * BLOCK), STEP * BLOCK)
+    def coef_copies(slot):
+        target = slot - lax.div(slot, GROUPS) * FOREIGN
+        rows = pl.ds(slot * (STEP * BLOCK), STEP * BLOCK)
         target_rows = pl.ds(target * (STEP * BLOCK), STEP * BLOCK)
         return [
             pltpu.make_async_remote_copy(
@@ -337,7 +346,7 @@
         ]
 
     def wall_copies(slot):
-        group = slot - lax.div(slot, GROUPS)
+        group = slot - lax.div(slot, GROUPS) * FOREIGN
         return [
             pltpu.make_async_remote_copy(
                 wall_out.at[slot], wall_in.at[me, group],
@@ -356,7 +365,8 @@
         wall_out[slot] = (first[:16] + (first[16:] + second))[:2]
 
     def solved_here(slot):
-        return (slot < GROUPS - 1) | ((slot == GROUPS - 1) & (depth > 0)) | ((slot == GROUPS) & (depth == 1))
+        own = (slot < GROUPS) & (slot < GROUPS - leaving)
+        return own | ((slot >= GROUPS) & (slot >= SLOTS - coming))
 
     def turn(a):
         return pltpu.roll(a, LOCAL, 1)
@@ -394,15 +404,16 @@
             return carry
 
         lax.fori_loop(0, QUARTER // UNROLL, some_modes, 0)
-        for k in range(GROUP // STEP):
-            for copy in coef_copies(group * (GROUP // STEP) + k):
-                copy.start()
+        for copy in coef_copies(group):
+            copy.start()
         wall_sums(group)
         for copy in wall_copies(group):
             copy.start()
 
     def solve_slot(turn, carry):
-        slot = turn + lax.div(turn, GROUPS - 1) * (1 - 2 * lax.rem(turn, GROUPS - 1))
+        late = lax.div(turn + FOREIGN, GROUPS)
+        later = lax.div(turn + FOREIGN, 2) + FOREIGN * (1 - lax.rem(turn + FOREIGN, 2))
+        slot = (1 - late) * turn + late * later
 
         @pl.when(solved_here(slot))
         def _():
@@ -410,7 +421,7 @@
 
         return carry
 
-    lax.fori_loop(0, GROUPS + 1, solve_slot, 0)
+    lax.fori_loop(0, SLOTS, solve_slot, 0)
 
     whole(sides, halo_send.at[0]).wait_send()
     whole(out_modes, mode_send.at[0]).wait_send()
@@ -436,8 +447,8 @@
         values = values * lax.rsqrt(total / grid + EPSILON)
         out_ref[e] = values.reshape(FIELDS, LOCAL, PTS)
 
-    row = lax.broadcasted_iota(jnp.int32, (4 * GROUP, 2 * PTS), 0)
-    lanes = lax.broadcasted_iota(jnp.int32, (4 * GROUP, 2 * PTS), 1)
+    row = lax.broadcasted_iota(jnp.int32, (4 * GROUP, SPAN), 0)
+    lanes = lax.broadcasted_iota(jnp.int32, (4 * GROUP, SPAN), 1)
     own = lax.div(lanes, QUARTER) == 2 * lax.div(row, 4) + lax.rem(row, 2)
     upper_wall = lax.rem(lax.div(row, 2), 2) == 0
 
@@ -448,10 +459,10 @@
             both = wall_in[q, group]
             parts.append(jnp.where(own, jnp.where(upper_wall, both[:1], both[1:]), 0.0))
         high, low = split(jnp.concatenate(parts, axis=1))
-        table = back[3 * MODES : 11 * MODES]
+        table = back[3 * MODES : 3 * MODES + 4 * SPAN]
         first = dot(jnp.concatenate([high, low], axis=0), table)
         count = 4 * GROUP
-        values = first[:count] + (first[count:] + dot(high, back[11 * MODES :]))
+        values = first[:count] + (first[count:] + dot(high, back[3 * MODES + 4 * SPAN :]))
         member = group * GROUP + lax.div(row[:, :PTS], 4)
         total = jnp.sum(jnp.where(lane == member, sum_mine[3], 0.0), axis=1, keepdims=True)
         values = values * lax.rsqrt(total / grid + EPSILON)
@@ -465,16 +476,14 @@
         for k in range(STEP):
             back_member(step * STEP + k)
 
-        @pl.when(lax.rem(step, 2) == 1)
-        def _():
-            wall_group(lax.div(step, 2))
-
+        wall_group(step)
         return carry
 
     lax.fori_loop(0, STEPS, back_step, 0)
 
     for held, here_now in (
-        (GROUPS - 1, depth == 0), (GROUPS + 1, depth == 1), (GROUPS, depth > 1)
+        (GROUPS - MOVED[0], depth == 0), (GROUPS - MOVED[1] + MOVED[0], depth == 1),
+        (GROUPS + MOVED[1], depth == 2), (GROUPS, depth > 2),
     ):
         @pl.when(here_now)
         def _():
@@ -499,7 +508,7 @@
     walls[1, :, 0] = np.where(k % 2 == 0, -curvature, curvature).reshape(4, LOCAL)
     weights = jnp.asarray(np.concatenate(split_table(walls.reshape(16, 8 * LOCAL)), axis=0))
     exchange = (4, MEMBERS * BLOCK, PTS)
-    larger = (4, (MEMBERS + GROUP) * BLOCK, PTS)
+    larger = (4, SLOTS * GROUP * BLOCK, PTS)
     rim = (2, MEMBERS, FIELDS, 32, PTS)
     vmem = pltpu.VMEM
     dma = pltpu.SemaphoreType.DMA
@@ -529,13 +538,13 @@
             vmem(exchange, F32),
             vmem((4, 1, PTS), F32),
             vmem((3, 8, 1, PTS), F32),
-            vmem((GROUPS + 1, 2, 2 * PTS), F32),
-            vmem((4, GROUPS + 1, 2, 2 * PTS), F32),
+            vmem((SLOTS, 2, SPAN), F32),
+            vmem((4, SLOTS, 2, SPAN), F32),
             dma((9,)),
             dma((1,)),
             dma((STEPS,)),
             dma((1,)),
-            dma((GROUPS + 1,)),
+            dma((SLOTS,)),
             dma((2,)),
             dma((STEPS,)),
             dma((3,)),

time: 63.4 us -> 62.6 us (0.987)
  Pallas kernels: 60.9 us -> 60.1 us
    pallas_call x1, Pallas kernels: 60.9 us -> 60.1 us  [per_device(): pl.pallas_call(functools.partial(kernel, sizes), out_shape=(pltpu.VMEM(st...]
where the time goes in v5:
time: 62.6 us; the launch traced here: 62.5 us
  Pallas kernels  60.1 us (96%)
  local copies, waits for them, and re-layouts  1.75 us (3%)
  between operations  0.64 us (1%)
    pallas_call x1, Pallas kernels, per_device(): pl.pallas_call(functools.partial(kernel, sizes), out_shape=(pltpu.VMEM(st...  60.1 us
    unnamed x2, local copies, waits for them, and re-layouts  1.75 us

profile of v5, /device:TPU:1, one launch (start us, length us, event | category | flops | bytes accessed | tf_op | source)
XLA Modules:
  0.0 62.5 jit_solution(13912407461556569720)
XLA Ops:
  0.6 60.1 %step.1 = (f32[12,4,64,128]{3,2,1,0:T(8,128)S(1)}, f32[12,2,2,128]{3,2,1,0:T(2,128)S(1)}) custom-call(f32[12,4,64,128]{3,2,1,0:T(8,128)} %state_hbm.1, f32[32,256,256]{2,1,0:T(8,128)} %inverse_hbm.1, bf16[512,256]{1,0:T(8,128)(2,1)} %constant.6.clone.project_hbm, bf16[1408,128]{1,0:T(8,128)(2,1)} %constant.7.clone.back_hbm, ...), custom_call_target="tpu_custom_call" | custom-call | tf_op jit(solution)/shard_map/step/pallas_call | solution.py:515
  60.8 1.1 %copy.9 = f32[12,4,64,128]{3,2,1,0:T(8,128)} copy(f32[12,4,64,128]{3,2,1,0:T(8,128)S(1)} %get-tuple-element.2) | data formatting | bytes 3145728
  61.9 0.6 copy.10

commit v6 on v5

--- a/solution.py
+++ b/solution.py
@@ -411,9 +411,10 @@
             copy.start()
 
     def solve_slot(turn, carry):
-        late = lax.div(turn + FOREIGN, GROUPS)
-        later = lax.div(turn + FOREIGN, 2) + FOREIGN * (1 - lax.rem(turn + FOREIGN, 2))
-        slot = (1 - late) * turn + late * later
+        def from_turn(n):
+            return lax.div(turn + SLOTS - n, SLOTS)
+
+        slot = turn + 3 * from_turn(3) - 4 * from_turn(4) + 3 * from_turn(5) - 5 * from_turn(7)
 
         @pl.when(solved_here(slot))
         def _():
@@ -508,7 +509,7 @@
     walls[1, :, 0] = np.where(k % 2 == 0, -curvature, curvature).reshape(4, LOCAL)
     weights = jnp.asarray(np.concatenate(split_table(walls.reshape(16, 8 * LOCAL)), axis=0))
     exchange = (4, MEMBERS * BLOCK, PTS)
-    larger = (4, SLOTS * GROUP * BLOCK, PTS)
+    larger = (4, SLOTS * GROUP * BLOCK + QUARTER, PTS)
     rim = (2, MEMBERS, FIELDS, 32, PTS)
     vmem = pltpu.VMEM
     dma = pltpu.SemaphoreType.DMA

time: 62.6 us -> 62.6 us (level)
  no operation moved by 1% of the time
where the time goes in v6:
time: 62.6 us; the launch traced here: 62.5 us
  Pallas kernels  60.1 us (96%)
  local copies, waits for them, and re-layouts  1.75 us (3%)
  between operations  0.64 us (1%)
    pallas_call x1, Pallas kernels, per_device(): pl.pallas_call(functools.partial(kernel, sizes), out_shape=(pltpu.VMEM(st...  60.1 us
    unnamed x2, local copies, waits for them, and re-layouts  1.75 us

profile of v6, /device:TPU:1, one launch (start us, length us, event | category | flops | bytes accessed | tf_op | source)
XLA Modules:
  0.0 62.5 jit_solution(8166088057155218647)
XLA Ops:
  0.6 60.1 %step.1 = (f32[12,4,64,128]{3,2,1,0:T(8,128)S(1)}, f32[12,2,2,128]{3,2,1,0:T(2,128)S(1)}) custom-call(f32[12,4,64,128]{3,2,1,0:T(8,128)} %state_hbm.1, f32[32,256,256]{2,1,0:T(8,128)} %inverse_hbm.1, bf16[512,256]{1,0:T(8,128)(2,1)} %constant.6.clone.project_hbm, bf16[1408,128]{1,0:T(8,128)(2,1)} %constant.7.clone.back_hbm, ...), custom_call_target="tpu_custom_call" | custom-call | tf_op jit(solution)/shard_map/step/pallas_call | solution.py:516
  60.8 1.1 %copy.9 = f32[12,4,64,128]{3,2,1,0:T(8,128)} copy(f32[12,4,64,128]{3,2,1,0:T(8,128)S(1)} %get-tuple-element.2) | data formatting | bytes 3145728
  61.9 0.6 copy.10
